TPU v7x, 32 devices: a whole 2x2x4 slice. The times are simulated.
32 devices in a mesh: wide: 16 (over z, y, x), narrow: 2 (over core).
Axes of the slice: x: 2, y: 2, z: 4, core: 2. Of those that a mesh axis runs over, the one named last changes fastest.
Arguments:
- qkv: float32 [3, 2, 1024, 1280], P(None, None, 'wide', 'narrow'), may hold values from -30 to 30
- eta: float32 [2, 1024], P('narrow', 'wide'), may hold values from 0.01 to 0.1
- fast_weights: float32 [2, 640, 3, 384], P('narrow', 'wide'), may hold values from -0.25 to 0.25
- momentum: float32 [2, 640, 3, 384], P('narrow', 'wide'), may hold values from -50 to 50
- ttt_gain: float32 [1280], P('narrow'), may hold values from 0.5 to 1.5
Outputs:
- mixed: float32 [2, 1024, 1280], P(None, 'wide', 'narrow')
- new_weights: float32 [2, 640, 3, 384], P('narrow', 'wide')
- new_momentum: float32 [2, 640, 3, 384], P('narrow', 'wide')
All inputs are finite; a program needn't handle non-finite values.
Results may differ from a plain program's by a relative error of at most 0.0003.
Values sent between devices are 32-bit elements; how exact they have to be, the bound alone decides.
A program may use at most 64 MiB of HBM per device.

v0:
```python
import math

import jax
import jax.numpy as jnp
import numpy as np
from jax import lax
from jax.sharding import PartitionSpec as P

D = 640
ATT = 128
WINDOW = 128


EPSILON = 1e-06
MOMENTUM_RATE = 0.9
STEP_SIZE = 0.03
PRECISION = lax.Precision.HIGHEST


def from_behind(block, axis, distance):
    devices = range(lax.axis_size(axis))
    route = [((i - distance) % len(devices), i) for i in devices]
    return lax.ppermute(block, axis, route)


def product(left, right):
    return jnp.dot(left, right, precision=PRECISION, preferred_element_type=jnp.float32)


def memory_read(inputs, weights):
    gate_pre = product(inputs, weights[:, 0, :])
    up_pre = product(inputs, weights[:, 1, :])
    hidden = jax.nn.silu(gate_pre) * up_pre
    return product(hidden, weights[:, 2, :].T)


def memory_gradient(key_rows, value_rows, rates, weights):
    gate_pre = product(key_rows, weights[:, 0, :])
    up_pre = product(key_rows, weights[:, 1, :])
    sigmoid = jax.nn.sigmoid(gate_pre)
    gated = gate_pre * sigmoid
    hidden = gated * up_pre
    weighted = rates[:, None] * value_rows
    back = -product(weighted, weights[:, 2, :])
    gate_back = back * up_pre * sigmoid * (1.0 + gate_pre * (1.0 - sigmoid))
    up_back = back * gated
    return (weighted, hidden, gate_back, up_back)


def renormalize(weights, moment):
    spread = jnp.sqrt(jnp.mean(moment * moment, axis=0) + EPSILON)
    moved = weights - STEP_SIZE * moment / spread
    ratio = jnp.sqrt(jnp.mean(weights * weights, axis=0) + EPSILON) / jnp.sqrt(
        jnp.mean(moved * moved, axis=0) + EPSILON
    )
    return moved * ratio


def window_attention(query_rows, key_rows, value_rows):
    groups, tok_rows, columns = query_rows.shape
    head_count = columns // ATT
    position = lax.axis_index("wide")
    reach = (WINDOW + tok_rows - 2) // tok_rows
    later_groups = jnp.arange(groups) >= 1
    key_parts, value_parts, offsets, live_parts = ([], [], [], [])
    for back in range(reach, 0, -1):
        keep = min(tok_rows, WINDOW - 1 - (back - 1) * tok_rows)
        got_keys, got_values = from_behind(
            (key_rows[:, tok_rows - keep :], value_rows[:, tok_rows - keep :]), "wide", back
        )
        same_group = position >= back
        key_parts.append(jnp.where(same_group, got_keys, jnp.roll(got_keys, 1, axis=0)))
        value_parts.append(jnp.where(same_group, got_values, jnp.roll(got_values, 1, axis=0)))
        offsets.append(np.arange(keep) + tok_rows - keep - back * tok_rows)
        live_parts.append(
            jnp.broadcast_to(jnp.logical_or(same_group, later_groups)[:, None], (groups, keep))
        )
    key_parts.append(key_rows)
    value_parts.append(value_rows)
    offsets.append(np.arange(tok_rows))
    live_parts.append(jnp.ones((groups, tok_rows), bool))
    near_keys = jnp.concatenate(key_parts, axis=1)
    near_values = jnp.concatenate(value_parts, axis=1)
    live = jnp.concatenate(live_parts, axis=1)
    offset = np.concatenate(offsets)
    distance = np.arange(tok_rows)[:, None] - offset[None, :]
    window_mask = jnp.asarray((distance >= 0) & (distance < WINDOW))
    allowed = live[:, None, None, :] & window_mask[None, None]
    span = near_keys.shape[1]
    queries4 = query_rows.reshape(groups, tok_rows, head_count, ATT)
    keys4 = near_keys.reshape(groups, span, head_count, ATT)
    values4 = near_values.reshape(groups, span, head_count, ATT)
    scores = jnp.einsum("cqhe,ckhe->chqk", queries4, keys4, precision=PRECISION) / math.sqrt(ATT)
    scores = jnp.where(allowed, scores, -1e30)
    highest = jnp.max(scores, axis=-1, keepdims=True)
    weights = jnp.exp(scores - highest)
    weights = weights / jnp.sum(weights, axis=-1, keepdims=True)
    output = jnp.einsum("chqk,ckhe->cqhe", weights, values4, precision=PRECISION)
    return output.reshape(groups, tok_rows, columns)


def local(qkv, eta, fast_weights, momentum, ttt_gain):
    query_rows, key_rows, value_rows = (qkv[0], qkv[1], qkv[2])
    attended = window_attention(query_rows, key_rows, value_rows)
    position = lax.axis_index("wide")
    readouts, updated_list, moment_list = ([], [], [])
    own_weights = fast_weights[0]
    own_moment = momentum[0]
    shard_rows = own_weights.shape[0]
    weights = lax.all_gather(own_weights, "wide", axis=0, tiled=True)
    moment_all = lax.all_gather(own_moment, "wide", axis=0, tiled=True)
    first_keys = key_rows[0, :, 0:D]
    first_values = value_rows[0, :, 0:D]
    first_read = memory_read(query_rows[0, :, 0:D], weights)
    weighted, hidden, gate_back, up_back = memory_gradient(
        first_keys, first_values, eta[0], weights
    )
    total = lax.psum(
        jnp.stack(
            [
                product(first_keys.T, gate_back),
                product(first_keys.T, up_back),
                -product(weighted.T, hidden),
            ],
            axis=1,
        ),
        "wide",
    )
    moment_all = MOMENTUM_RATE * moment_all + total
    updated = renormalize(weights, moment_all)
    new_own = lax.dynamic_slice_in_dim(updated, position * shard_rows, shard_rows, 0)
    new_moment = lax.dynamic_slice_in_dim(moment_all, position * shard_rows, shard_rows, 0)
    second_read = memory_read(query_rows[1, :, 0:D], updated)
    readouts.append(jnp.stack([first_read, second_read]))
    updated_list.append(new_own)
    moment_list.append(new_moment)
    readout = readouts[0]
    squares = lax.psum(jnp.sum(readout * readout, axis=-1), "narrow")
    full_width = readout.shape[-1] * lax.axis_size("narrow")
    scale = jnp.sqrt(squares / full_width + EPSILON)
    mixed = attended + ttt_gain * (readout / scale[..., None])
    return (mixed, jnp.stack(updated_list), jnp.stack(moment_list))


def solution(mesh):
    return jax.shard_map(
        local,
        mesh=mesh,
        in_specs=(
            P(None, None, "wide", "narrow"),
            P("narrow", "wide"),
            P("narrow", "wide", None, None),
            P("narrow", "wide", None, None),
            P("narrow"),
        ),
        out_specs=(
            P(None, "wide", "narrow"),
            P("narrow", "wide", None, None),
            P("narrow", "wide", None, None),
        ),
        check_vma=False,
    )
```

profile of v0, /device:TPU:0, one launch (start us, length us, event | category | flops | bytes accessed | tf_op | source)
XLA Modules:
  0.0 339.0 jit_solution(4695409853012924320)
XLA Ops:
  7.2 1.8 copy.33
  9.1 1.8 copy.35
  10.9 2.1 fusion.63
  13.1 3.0 collective-permute-start.3
  16.0 1.7 slice.112
  17.8 1.5 collective-permute-start.2
  20.8 1.7 slice.107
  22.5 1.5 collective-permute-start
  27.1 74.0 %all-gather.5.cloned.1.call-done = f32[1,640,3,384]{3,0,2,1:T(1,128)} async-done(((f32[1,40,3,384]{3,0,2,1:T(1,128)}), f32[1,640,3,384]{3,0,2,1:T(1,128)}) %all-gather.5.cloned.1.call-update) | async-done | bytes 2949136 | tf_op jit(solution)/shard_map/all_gather | solution.py:110
  101.1 5.7 %copy.34 = f32[1,640,3,384]{1,3,2,0:T(8,128)S(1)} copy(f32[1,640,3,384]{3,0,2,1:T(1,128)} %all-gather.5.cloned.1.call-done) | data formatting | bytes 5898240 | tf_op jit(solution)/shard_map/all_gather | solution.py:110
  106.8 2.1 fusion.14
  108.9 2.0 fusion.16
  111.0 1.9 fusion
  116.1 1.8 pad_maximum_fusion
  124.0 3.3 fusion.68
  130.1 39.3 %all-gather.7.cloned.1.call-done = f32[1,640,3,384]{3,0,2,1:T(1,128)} async-done(((f32[1,40,3,384]{3,0,2,1:T(1,128)}), f32[1,640,3,384]{3,0,2,1:T(1,128)}) %all-gather.7.cloned.1.call-update) | async-done | bytes 2949136 | tf_op jit(solution)/shard_map/all_gather | solution.py:111
  169.4 7.1 %copy.36 = f32[1,640,3,384]{1,3,2,0:T(8,128)} copy(f32[1,640,3,384]{3,0,2,1:T(1,128)} %all-gather.7.cloned.1.call-done) | data formatting | bytes 5898240 | tf_op jit(solution)/shard_map/all_gather | solution.py:111
  176.5 2.0 fusion.15
  178.5 2.1 convolution_multiply_fusion.1
  181.4 136.0 %all-reduce.2.cloned.1.call-done = f32[640,3,384]{0,2,1:T(8,128)} async-done(((f32[640,3,384]{0,2,1:T(8,128)}), f32[640,3,384]{0,2,1:T(8,128)}) %all-reduce.2.cloned.1.call-update) | async-done | bytes 2949136 | tf_op jit(solution)/shard_map/psum | solution.py:118
  317.3 3.2 multiply_reduce_fusion.2
  322.0 2.1 convolution_bitcast_fusion.6
  324.5 2.1 fusion.3
  327.4 2.5 psum.15
  (64 shorter events, 22.6 us)
Async XLA Ops:
  7.2 16.9 %copy-start.2 = (pred[64,191]{1,0:T(32,128)(4,1)S(1)}, pred[64,191]{1,0:T(32,128)(4,1)}, u32[]{:S(2)}) copy-start(pred[64,191]{1,0:T(32,128)(4,1)} %constant.50.clone) | copy-start | bytes 36676
  7.2 93.9 %all-gather.5.cloned.1.call-start = ((), (), s32[]{:S(2)}) async-start(), calls=%async_computation.1 | async-start | bytes 3133440 | tf_op jit(solution)/shard_map/all_gather | solution.py:110
  9.0 160.4 %all-gather.7.cloned.1.call-start = ((), (), s32[]{:S(2)}) async-start(), calls=%async_computation.2 | async-start | bytes 3133440 | tf_op jit(solution)/shard_map/all_gather | solution.py:111
  10.9 306.4 %all-reduce.2.cloned.1.call-start = ((), (), s32[]{:S(2)}) async-start(), calls=%async_computation | async-start | bytes 5898240 | tf_op jit(solution)/shard_map/psum | solution.py:118
  13.1 109.8 %collective-permute-start.3 = (f32[2,64,640]{2,1,0:T(8,128)}, f32[2,64,640]{2,1,0:T(8,128)}, u32[]{:S(2)}, u32[]{:S(2)}) collective-permute-start(f32[2,64,640]{2,1,0:T(8,128)} %get-tuple-element.9), channel_id=1, source_target_pairs={{30,0},{0,2},{2,4},{4,6},{6,8},{8,10},{10,12},{12,14},{14,16},{16,... | collective-permute-start | bytes 983048 | tf_op jit(solution)/shard_map/ppermute | solution.py:23
  17.8 100.2 %collective-permute-start.2 = (f32[2,63,640]{2,1,0:T(8,128)}, f32[2,63,640]{2,1,0:T(8,128)S(1)}, u32[]{:S(2)}, u32[]{:S(2)}) collective-permute-start(f32[2,63,640]{2,1,0:T(8,128)} %slice.112), channel_id=1, source_target_pairs={{28,0},{30,2},{0,4},{2,6},{4,8},{6,10},{8,12},{10,14},{12,16},{14,... | collective-permute-start | bytes 967688 | tf_op jit(solution)/shard_map/ppermute | solution.py:23
  19.3 108.3 %collective-permute-start.1 = (f32[2,64,640]{2,1,0:T(8,128)}, f32[2,64,640]{2,1,0:T(8,128)}, u32[]{:S(2)}, u32[]{:S(2)}) collective-permute-start(f32[2,64,640]{2,1,0:T(8,128)} %get-tuple-element.8), channel_id=1, source_target_pairs={{30,0},{0,2},{2,4},{4,6},{6,8},{8,10},{10,12},{12,14},{14,16},{16,... | collective-permute-start | bytes 983048 | tf_op jit(solution)/shard_map/ppermute | solution.py:23
  22.5 95.5 %collective-permute-start = (f32[2,63,640]{2,1,0:T(8,128)}, f32[2,63,640]{2,1,0:T(8,128)}, u32[]{:S(2)}, u32[]{:S(2)}) collective-permute-start(f32[2,63,640]{2,1,0:T(8,128)} %slice.107), channel_id=1, source_target_pairs={{28,0},{30,2},{0,4},{2,6},{4,8},{6,10},{8,12},{10,14},{12,16},{14,... | collective-permute-start | bytes 967688 | tf_op jit(solution)/shard_map/ppermute | solution.py:23
  27.1 83.9 %copy-start.4 = (f32[1,64]{1,0:T(1,128)S(1)}, f32[1,64]{1,0:T(1,128)}, u32[]{:S(2)}) copy-start(f32[1,64]{1,0:T(1,128)} %param.7) | copy-start | bytes 772
  106.8 6.1 %copy-start = (f32[3,2,64,640]{3,2,1,0:T(8,128)S(1)}, f32[3,2,64,640]{3,2,1,0:T(8,128)}, u32[]{:S(2)}) copy-start(f32[3,2,64,640]{3,2,1,0:T(8,128)} %param.6) | copy-start | bytes 2949124
  122.9 5.9 %copy-start.1 = (f32[2,64,5,128]{3,1,2,0:T(8,128)S(1)}, f32[2,64,5,128]{3,1,2,0:T(8,128)}, u32[]{:S(2)}) copy-start(f32[2,64,5,128]{3,1,2,0:T(8,128)} %copy.27) | copy-start | bytes 983044
  324.3 7.4 %copy-start.3 = (f32[640]{0:T(1024)S(1)}, f32[640]{0:T(1024)}, u32[]{:S(2)}) copy-start(f32[640]{0:T(1024)} %param.10) | copy-start | bytes 7684
Sparse Core Ops, SparseCore 0:
  11.4 89.6 all-gather.4
  104.4 64.9 all-gather.6
  175.1 142.1 all-reduce.1
where the time goes:
time: 340 us; the launch traced here: 339 us
  waiting for transfers between devices  249 us (73%)
  local copies, waits for them, and re-layouts  33.1 us (10%)
  matrix products  23.6 us (7%)
  between operations  14 us (4%)
  other arithmetic  8.83 us (3%)
  starting transfers between devices  7.62 us (2%)
    psum x1, waiting for transfers between devices, local(): lax.psum(jnp.stack([product(first_keys.T, gate_back), product(first_keys....  136 us
    all_gather x1, waiting for transfers between devices, local(): weights = lax.all_gather(own_weights, 'wide', axis=0, tiled=True)  74 us
    all_gather x1, waiting for transfers between devices, local(): moment_all = lax.all_gather(own_moment, 'wide', axis=0, tiled=True)  39.3 us
    dot_general x12, matrix products, product(): jnp.dot(left, right, precision=PRECISION, preferred_element_type=jnp.floa...  18.9 us
    ppermute x4, starting transfers between devices, from_behind(): return lax.ppermute(block, axis, route)  7.5 us
    all_gather x1, local copies, waits for them, and re-layouts, local(): moment_all = lax.all_gather(own_moment, 'wide', axis=0, tiled=True)  7.07 us
  transfers between devices with their start and end apart: 7, of which 3 were waited for; matrix products, arithmetic and copies ran while one was open for 15% of the time, Pallas kernels for 0%

commit v1 on v0

v1 whole, which is shorter than its diff:
```python
import functools
import math

import jax
import jax.numpy as jnp
from jax import lax
from jax.experimental import pallas as pl
from jax.experimental.pallas import tpu as pltpu
from jax.sharding import PartitionSpec as P

ATT = 128
WINDOW = 128
LANES = 128
EPSILON = 1e-06
MOMENTUM_RATE = 0.9
STEP_SIZE = 0.03
MESH = pl.DeviceIdType.MESH
F32 = jnp.float32
BF16 = jnp.bfloat16


def contract(left, right, on_left, on_right, precision=None):
    dims = (((on_left,), (on_right,)), ((), ()))
    return lax.dot_general(left, right, dims, precision=precision, preferred_element_type=F32)


def split(value):
    high = value.astype(BF16)
    return high, (value - high.astype(F32)).astype(BF16)


def times(value, high_ref, low_ref, which, on=0):
    rows = value.shape[0]
    high, low = split(value)
    both = contract(jnp.concatenate([high, low], axis=0), high_ref[which], 1, on)
    return both[:rows] + both[rows:] + contract(high, low_ref[which], 1, on)


def token_sum(left, right):
    high = left.astype(BF16).astype(F32)
    stacked = jnp.concatenate([high, high, left - high], axis=0).T.astype(BF16)
    right_high, right_low = split(right)
    return contract(stacked, jnp.concatenate([right_high, right_low, right_high], axis=0), 1, 0)


def kernel(n, plane, width, part, reach, qkv, eta, own_w, own_m, gain, mixed, new_w, new_m,
           wg, mg, grad, ra, rb, sa, sb, ra2, rb2, wfull, whi, wlo, halo, squares, read0,
           wsem, msem, a1, b1, a2, b2, hsem, qsem, ssem):
    layers = n // plane
    chunks, rows, _ = own_w.shape
    per = chunks // 3
    groups, tok = qkv.shape[1], qkv.shape[2]
    columns = qkv.shape[3]
    me = lax.axis_index("wide")
    mine = lax.axis_index("narrow")
    z, p = me // plane, me % plane
    pa, pb = pl.ds(0, part), pl.ds(part, chunks - part)

    def at(zz, pp):
        return ((zz + layers) % layers) * plane + (pp + plane) % plane

    zs, ps = range(1, layers), range(1, plane)
    started = []

    def send(src, dst, sem, target):
        copy = pltpu.make_async_remote_copy(
            src_ref=src, dst_ref=dst, send_sem=ssem.at[len(started)], recv_sem=sem,
            device_id=target, device_id_type=MESH)
        copy.start()
        started.append(copy)

    def arrived(dst, sem):
        pltpu.make_async_remote_copy(
            src_ref=dst, dst_ref=dst, send_sem=ssem.at[0], recv_sem=sem,
            device_id={"wide": at(z, p + 1)}, device_id_type=MESH).wait_recv()

    barrier = pltpu.get_barrier_semaphore()
    friends = [{"wide": at(z + d, p)} for d in zs] + [{"wide": at(z, p + d)} for d in ps]
    for back in range(1, reach + 1):
        friends += [{"wide": (me + back) % n}, {"wide": (me + n - back) % n}]
    friends += [{"narrow": (mine + d) % width} for d in range(1, width)]
    for friend in friends:
        pl.semaphore_signal(barrier, inc=1, device_id=friend, device_id_type=MESH)
    pl.semaphore_wait(barrier, len(friends))

    def gather_start(own, buf, sem):
        for d in zs:
            send(own.at[pa], buf.at[me, pa], sem.at[0, me], {"wide": at(z + d, p)})
        for d in ps:
            send(own.at[pb], buf.at[me, pb], sem.at[1, me], {"wide": at(z, p + d)})
        for d in ps:
            send(own.at[pa], buf.at[me, pa], sem.at[0, me], {"wide": at(z, p + d)})
        for d in zs:
            send(own.at[pb], buf.at[me, pb], sem.at[1, me], {"wide": at(z + d, p)})

    def gather_finish(buf, sem):
        for d in range(1, max(layers, plane)):
            if d < layers:
                j = at(z - d, p)
                arrived(buf.at[j, pa], sem.at[0, j])
                for e in ps:
                    send(buf.at[j, pa], buf.at[j, pa], sem.at[0, j], {"wide": at(z, p + e)})
            if d < plane:
                j = at(z, p - d)
                arrived(buf.at[j, pb], sem.at[1, j])
                for e in zs:
                    send(buf.at[j, pb], buf.at[j, pb], sem.at[1, j], {"wide": at(z + e, p)})
        for dz in range(layers):
            for dp in range(plane):
                j = at(z - dz, p - dp)
                if dp:
                    arrived(buf.at[j, pa], sem.at[0, j])
                if dz:
                    arrived(buf.at[j, pb], sem.at[1, j])

    def place(buf, dst):
        for j in range(n):
            for c in range(chunks):
                lane = (c % per) * LANES
                dst[c // per, j * rows:(j + 1) * rows, lane:lane + LANES] = buf[j, c]

    def attend(c):
        def head(h, carry):
            lane = pl.ds(pl.multiple_of(h * ATT, ATT), ATT)
            keys, values, live = [], [], []
            for back in range(reach, 0, -1):
                wraps = jnp.where(me >= back, 0, 1)
                source = (c + groups - wraps) % groups
                keys.append(halo[back - 1, 0, source, :, lane])
                values.append(halo[back - 1, 1, source, :, lane])
            keys.append(qkv[1, c, :, lane])
            values.append(qkv[2, c, :, lane])
            keys, values = jnp.concatenate(keys, axis=0), jnp.concatenate(values, axis=0)
            span = keys.shape[0]
            scores = contract(qkv[0, c, :, lane], keys, 1, 1, lax.Precision.HIGHEST)
            scores = scores / math.sqrt(ATT)
            spot = lax.broadcasted_iota(jnp.int32, (tok, span), 1) - reach * tok
            distance = lax.broadcasted_iota(jnp.int32, (tok, span), 0) - spot
            first = -(c * n + me) * tok
            allowed = (distance >= 0) & (distance < WINDOW) & (spot >= first)
            scores = jnp.where(allowed, scores, -1e30)
            weights = jnp.exp(scores - jnp.max(scores, axis=-1, keepdims=True))
            weights = weights / jnp.sum(weights, axis=-1, keepdims=True)
            mixed[c, :, lane] = contract(weights, values, 1, 0, lax.Precision.HIGHEST)
            return carry

        lax.fori_loop(0, columns // ATT, head, 0)

    def read(value):
        gate, up = times(value, whi, wlo, 0), times(value, whi, wlo, 1)
        return times(gate / (1.0 + jnp.exp(-gate)) * up, whi, wlo, 2, 1)

    def share(c, readout):
        total = jnp.sum(readout * readout, axis=-1, keepdims=True)
        squares[c, mine] = jnp.broadcast_to(total, (tok, LANES))
        for d in range(1, width):
            send(squares.at[c, mine], squares.at[c, mine], qsem.at[c, mine],
                 {"narrow": (mine + d) % width})

    def mix(c, readout):
        for d in range(1, width):
            other = (mine + d) % width
            arrived(squares.at[c, other], qsem.at[c, other])
        total = squares[c, 0]
        for d in range(1, width):
            total = total + squares[c, d]
        scale = jnp.sqrt(total[:, :1] / (columns * width) + EPSILON)
        mixed[c] = mixed[c] + gain[...] * (readout / scale)

    gather_start(own_w, wg, wsem)
    wg[me] = own_w[...]
    gather_finish(wg, wsem)
    for back in range(1, reach + 1):
        for kind in range(2):
            send(qkv.at[1 + kind], halo.at[back - 1, kind], hsem.at[back - 1, kind],
                 {"wide": (me + back) % n})
    place(wg, wfull)
    for m in range(3):
        whi[m], wlo[m] = split(wfull[m])

    key_rows = qkv[1, 0]
    gate, up = times(key_rows, whi, wlo, 0), times(key_rows, whi, wlo, 1)
    sigmoid = 1.0 / (1.0 + jnp.exp(-gate))
    gated = gate * sigmoid
    weighted = eta[...] * qkv[2, 0]
    back_rows = -times(weighted, whi, wlo, 2)
    gate_back = back_rows * up * sigmoid * (1.0 + gate * (1.0 - sigmoid))
    sums = ((key_rows, gate_back), (key_rows, back_rows * gated), (-weighted, gated * up))
    for m, (left, right) in enumerate(sums):
        total = token_sum(left, right)
        for c in range(per):
            for j in range(n):
                grad[j, m * per + c] = total[j * rows:(j + 1) * rows, c * LANES:(c + 1) * LANES]

    for d in range(1, max(layers, plane)):
        if d < plane:
            for e in range(1, layers + 1):
                zz = (z + e) % layers
                send(grad.at[at(zz, p + d), pa], ra.at[d - 1, zz], a1.at[d - 1, zz],
                     {"wide": at(z, p + d)})
        if d < layers:
            for e in range(1, plane + 1):
                pp = (p + e) % plane
                send(grad.at[at(z + d, pp), pb], rb.at[d - 1, pp], b1.at[d - 1, pp],
                     {"wide": at(z + d, p)})

    for back in range(reach):
        for kind in range(2):
            arrived(halo.at[back, kind], hsem.at[back, kind])
    attend(0)

    def half_a(zz):
        total = grad[at(zz, p), pa]
        for d in ps:
            arrived(ra.at[d - 1, zz], a1.at[d - 1, zz])
            total = total + ra[d - 1, zz]
        return total

    def half_b(pp):
        total = grad[at(z, pp), pb]
        for d in zs:
            arrived(rb.at[d - 1, pp], b1.at[d - 1, pp])
            total = total + rb[d - 1, pp]
        return total

    for d in range(1, max(layers, plane)):
        if d < layers:
            sa[d - 1] = half_a((z + d) % layers)
        if d < plane:
            sb[d - 1] = half_b((p + d) % plane)
        if d < layers:
            send(sa.at[d - 1], ra2.at[d - 1], a2.at[d - 1], {"wide": at(z + d, p)})
        if d < plane:
            send(sb.at[d - 1], rb2.at[d - 1], b2.at[d - 1], {"wide": at(z, p + d)})
    new_m[pa] = MOMENTUM_RATE * own_m[pa] + half_a(z)
    new_m[pb] = MOMENTUM_RATE * own_m[pb] + half_b(p)
    for g in range(1, groups):
        attend(g)
    for d in zs:
        arrived(ra2.at[d - 1], a2.at[d - 1])
        new_m[pa] = new_m[pa] + ra2[d - 1]
    for d in ps:
        arrived(rb2.at[d - 1], b2.at[d - 1])
        new_m[pb] = new_m[pb] + rb2[d - 1]
    mg[me] = new_m[...]

    gather_start(new_m, mg, msem)
    first_read = read(qkv[0, 0])
    read0[...] = first_read
    share(0, first_read)
    gather_finish(mg, msem)
    mix(0, read0[...])

    for m in range(3):
        for c in range(m * per, (m + 1) * per):
            lane = pl.ds((c % per) * LANES, LANES)
            weights = wfull[m, :, lane]
            moment = mg[:, c]
            spread = jnp.sqrt(jnp.sum(jnp.sum(moment * moment, axis=0), axis=0, keepdims=True)
                              / columns + EPSILON)
            pull = STEP_SIZE / spread
            stay = wg[:, c] - moment * pull[None]
            ratio = jnp.sqrt(jnp.mean(weights * weights, axis=0, keepdims=True) + EPSILON)
            ratio = ratio / jnp.sqrt(
                jnp.sum(jnp.sum(stay * stay, axis=0), axis=0, keepdims=True) / columns + EPSILON)
            new_w[c] = (own_w[c] - new_m[c] * pull) * ratio
            for j in range(n):
                moved = (wg[j, c] - mg[j, c] * pull) * ratio
                wfull[m, j * rows:(j + 1) * rows, lane] = moved
        whi[m], wlo[m] = split(wfull[m])
    for g in range(1, groups):
        later = read(qkv[0, g])
        share(g, later)
        mix(g, later)
    for copy in started:
        copy.wait_send()


def local(n, width, qkv, eta, fast_weights, momentum, ttt_gain):
    groups, tok, columns = qkv.shape[1:]
    _, rows, three, hidden = fast_weights.shape
    per = hidden // LANES
    chunks = three * per
    part = (chunks + 1) // 2
    rest = chunks - part
    plane = 4 if n % 4 == 0 else 1
    layers = n // plane
    reach = (WINDOW + tok - 2) // tok

    def blocks(value):
        value = value[0].reshape(rows, chunks, LANES)
        return jnp.transpose(value, (1, 0, 2))

    def unblocks(value):
        return jnp.transpose(value, (1, 0, 2)).reshape(1, rows, three, hidden)

    zs, ps = layers - 1, plane - 1
    sends = 2 * (zs + ps + 2 * zs * ps) + 2 * zs + 2 * ps
    sends += ps * layers + zs * plane + zs + ps + 2 * reach + groups * (width - 1)
    vmem, dma = pltpu.VMEM, pltpu.SemaphoreType.DMA
    block = jax.ShapeDtypeStruct((chunks, rows, LANES), F32)
    mixed, new_w, new_m = pl.pallas_call(
        functools.partial(kernel, n, plane, width, part, reach),
        out_shape=(jax.ShapeDtypeStruct((groups, tok, columns), F32), block, block),
        in_specs=[pl.BlockSpec(memory_space=vmem)] * 5,
        out_specs=(pl.BlockSpec(memory_space=vmem),) * 3,
        scratch_shapes=[
            vmem((n, chunks, rows, LANES), F32),
            vmem((n, chunks, rows, LANES), F32),
            vmem((n, chunks, rows, LANES), F32),
            vmem((ps, layers, part, rows, LANES), F32),
            vmem((zs, plane, rest, rows, LANES), F32),
            vmem((zs, part, rows, LANES), F32),
            vmem((ps, rest, rows, LANES), F32),
            vmem((zs, part, rows, LANES), F32),
            vmem((ps, rest, rows, LANES), F32),
            vmem((3, columns, hidden), F32),
            vmem((3, columns, hidden), BF16),
            vmem((3, columns, hidden), BF16),
            vmem((reach, 2, groups, tok, columns), F32),
            vmem((groups, width, tok, LANES), F32),
            vmem((tok, columns), F32),
            dma((2, n)), dma((2, n)),
            dma((ps, layers)), dma((zs, plane)), dma((zs,)), dma((ps,)),
            dma((reach, 2)), dma((groups, width)), dma((sends,)),
        ],
        compiler_params=pltpu.CompilerParams(
            collective_id=0, has_side_effects=True, vmem_limit_bytes=60 * 1024 * 1024),
    )(qkv, eta.reshape(tok, 1), blocks(fast_weights), blocks(momentum),
      ttt_gain.reshape(1, columns))
    return mixed, unblocks(new_w), unblocks(new_m)


def solution(mesh):
    return jax.shard_map(
        functools.partial(local, mesh.shape["wide"], mesh.shape["narrow"]),
        mesh=mesh,
        in_specs=(
            P(None, None, "wide", "narrow"),
            P("narrow", "wide"),
            P("narrow", "wide", None, None),
            P("narrow", "wide", None, None),
            P("narrow"),
        ),
        out_specs=(
            P(None, "wide", "narrow"),
            P("narrow", "wide", None, None),
            P("narrow", "wide", None, None),
        ),
        check_vma=False,
    )
```

time: 340 us -> 180 us (0.53)
  the two profiles are of different devices: /device:TPU:0 before, /device:TPU:7 now
where the time goes in v1:
time: 180 us
  Pallas kernels  170 us (94%)
  local copies, waits for them, and re-layouts  8.84 us (5%)
    pallas_call x1, Pallas kernels, local(): pl.pallas_call(functools.partial(kernel, n, plane, width, part, reach), o...  170 us
    unnamed x13, local copies, waits for them, and re-layouts  4.6 us

profile of v1, /device:TPU:7, one launch (start us, length us, event | category | flops | bytes accessed | tf_op | source)
XLA Modules:
  0.0 180.0 jit_solution(9137197647776477997)
XLA Ops:
  0.6 0.0 copy-start.3
  0.6 1.3 reshape.19.gain
  1.9 0.0 copy-done.3
  1.9 0.7 copy.13.eta
  2.6 1.0 copy.9
  3.6 0.0 copy-start.1
  3.6 0.1 reshape_squeeze.6
  3.7 0.8 copy-done.1
  4.5 0.1 copy.11
  4.6 0.1 reshape_squeeze.7
  4.7 0.8 copy_bitcast_fusion
  5.6 170.5 %shard_map.76 = (f32[2,64,640]{2,1,0:T(8,128)}, f32[9,40,128]{2,1,0:T(8,128)}, f32[9,40,128]{2,1,0:T(8,128)}) custom-call(f32[3,2,64,640]{3,2,1,0:T(8,128)} %qkv.1, f32[64,1]{1,0:T(8,128)} %copy.13.eta, f32[9,40,128]{2,1,0:T(8,128)} %get-tuple-element.13.own_w, f32[9,40,128]{2,1,0:T(8,128)} %get-tuple-element.12.own_m, f32[1,640]{1,0:T(1,128)} %reshape.19.gain), custom_call_target="tpu_custom_call" | custom-call | tf_op jit(solution)/shard_map/pallas_call | solution.py:302
  176.0 1.0 copy.14
  177.0 0.1 reshape.20
  177.1 0.0 copy-start.2
  177.1 0.7 copy.16
  177.8 0.3 copy-done.2
  178.1 0.1 copy.15
  178.2 0.1 reshape.21
  178.3 0.0 copy-start
  178.3 0.7 copy.17
  179.0 0.3 copy-done
  179.3 0.7 copy.21
Async XLA Ops:
  0.6 1.3 copy-start.3
  3.6 0.9 copy-start.1
  177.1 1.0 copy-start.2
  178.3 1.0 copy-start

commit v2 on v1

--- a/solution.py
+++ b/solution.py
@@ -83,6 +83,15 @@
         pl.semaphore_signal(barrier, inc=1, device_id=friend, device_id_type=MESH)
     pl.semaphore_wait(barrier, len(friends))
 
+    def lend(g):
+        for back in range(1, reach + 1):
+            send(qkv.at[pl.ds(1, 2), g], halo.at[back - 1, g], hsem.at[back - 1, g],
+                 {"wide": (me + back) % n})
+
+    def borrow(g):
+        for back in range(reach):
+            arrived(halo.at[back, g], hsem.at[back, g])
+
     def gather_start(own, buf, sem):
         for d in zs:
             send(own.at[pa], buf.at[me, pa], sem.at[0, me], {"wide": at(z + d, p)})
@@ -93,7 +102,7 @@
         for d in zs:
             send(own.at[pb], buf.at[me, pb], sem.at[1, me], {"wide": at(z + d, p)})
 
-    def gather_finish(buf, sem):
+    def gather_finish(buf, sem, after):
         for d in range(1, max(layers, plane)):
             if d < layers:
                 j = at(z - d, p)
@@ -105,6 +114,8 @@
                 arrived(buf.at[j, pb], sem.at[1, j])
                 for e in zs:
                     send(buf.at[j, pb], buf.at[j, pb], sem.at[1, j], {"wide": at(z + e, p)})
+        for g in after:
+            lend(g)
         for dz in range(layers):
             for dp in range(plane):
                 j = at(z - dz, p - dp)
@@ -124,10 +135,10 @@
             lane = pl.ds(pl.multiple_of(h * ATT, ATT), ATT)
             keys, values, live = [], [], []
             for back in range(reach, 0, -1):
-                wraps = jnp.where(me >= back, 0, 1)
-                source = (c + groups - wraps) % groups
-                keys.append(halo[back - 1, 0, source, :, lane])
-                values.append(halo[back - 1, 1, source, :, lane])
+                wraps = jnp.where(me >= back, 0, min(c, 1))
+                source = c - wraps
+                keys.append(halo[back - 1, source, 0, :, lane])
+                values.append(halo[back - 1, source, 1, :, lane])
             keys.append(qkv[1, c, :, lane])
             values.append(qkv[2, c, :, lane])
             keys, values = jnp.concatenate(keys, axis=0), jnp.concatenate(values, axis=0)
@@ -169,11 +180,7 @@
 
     gather_start(own_w, wg, wsem)
     wg[me] = own_w[...]
-    gather_finish(wg, wsem)
-    for back in range(1, reach + 1):
-        for kind in range(2):
-            send(qkv.at[1 + kind], halo.at[back - 1, kind], hsem.at[back - 1, kind],
-                 {"wide": (me + back) % n})
+    gather_finish(wg, wsem, (0,))
     place(wg, wfull)
     for m in range(3):
         whi[m], wlo[m] = split(wfull[m])
@@ -204,9 +211,7 @@
                 send(grad.at[at(z + d, pp), pb], rb.at[d - 1, pp], b1.at[d - 1, pp],
                      {"wide": at(z + d, p)})
 
-    for back in range(reach):
-        for kind in range(2):
-            arrived(halo.at[back, kind], hsem.at[back, kind])
+    borrow(0)
     attend(0)
 
     def half_a(zz):
@@ -234,8 +239,6 @@
             send(sb.at[d - 1], rb2.at[d - 1], b2.at[d - 1], {"wide": at(z, p + d)})
     new_m[pa] = MOMENTUM_RATE * own_m[pa] + half_a(z)
     new_m[pb] = MOMENTUM_RATE * own_m[pb] + half_b(p)
-    for g in range(1, groups):
-        attend(g)
     for d in zs:
         arrived(ra2.at[d - 1], a2.at[d - 1])
         new_m[pa] = new_m[pa] + ra2[d - 1]
@@ -248,7 +251,7 @@
     first_read = read(qkv[0, 0])
     read0[...] = first_read
     share(0, first_read)
-    gather_finish(mg, msem)
+    gather_finish(mg, msem, range(1, groups))
     mix(0, read0[...])
 
     for m in range(3):
@@ -271,6 +274,8 @@
     for g in range(1, groups):
         later = read(qkv[0, g])
         share(g, later)
+        borrow(g)
+        attend(g)
         mix(g, later)
     for copy in started:
         copy.wait_send()
@@ -281,7 +286,7 @@
     _, rows, three, hidden = fast_weights.shape
     per = hidden // LANES
     chunks = three * per
-    part = (chunks + 1) // 2
+    part = 7 * chunks // 9
     rest = chunks - part
     plane = 4 if n % 4 == 0 else 1
     layers = n // plane
@@ -296,7 +301,7 @@
 
     zs, ps = layers - 1, plane - 1
     sends = 2 * (zs + ps + 2 * zs * ps) + 2 * zs + 2 * ps
-    sends += ps * layers + zs * plane + zs + ps + 2 * reach + groups * (width - 1)
+    sends += ps * layers + zs * plane + zs + ps + groups * reach + groups * (width - 1)
     vmem, dma = pltpu.VMEM, pltpu.SemaphoreType.DMA
     block = jax.ShapeDtypeStruct((chunks, rows, LANES), F32)
     mixed, new_w, new_m = pl.pallas_call(
@@ -317,12 +322,12 @@
             vmem((3, columns, hidden), F32),
             vmem((3, columns, hidden), BF16),
             vmem((3, columns, hidden), BF16),
-            vmem((reach, 2, groups, tok, columns), F32),
+            vmem((reach, groups, 2, tok, columns), F32),
             vmem((groups, width, tok, LANES), F32),
             vmem((tok, columns), F32),
             dma((2, n)), dma((2, n)),
             dma((ps, layers)), dma((zs, plane)), dma((zs,)), dma((ps,)),
-            dma((reach, 2)), dma((groups, width)), dma((sends,)),
+            dma((reach, groups)), dma((groups, width)), dma((sends,)),
         ],
         compiler_params=pltpu.CompilerParams(
             collective_id=0, has_side_effects=True, vmem_limit_bytes=60 * 1024 * 1024),

time: 180 us -> 150 us (0.83)
  the two profiles are of different devices: /device:TPU:7 before, /device:TPU:0 now
where the time goes in v2:
time: 150 us; the launch traced here: 148 us
  Pallas kernels  139 us (93%)
  local copies, waits for them, and re-layouts  8.84 us (6%)
    pallas_call x1, Pallas kernels, local(): pl.pallas_call(functools.partial(kernel, n, plane, width, part, reach), o...  139 us
    unnamed x13, local copies, waits for them, and re-layouts  4.6 us

profile of v2, /device:TPU:0, one launch (start us, length us, event | category | flops | bytes accessed | tf_op | source)
XLA Modules:
  0.0 148.3 jit_solution(12581465612733278663)
XLA Ops:
  0.6 0.0 copy-start.3
  0.6 1.3 reshape.19.gain
  1.9 0.0 copy-done.3
  1.9 0.7 copy.13.eta
  2.6 1.0 copy.9
  3.6 0.0 copy-start.1
  3.6 0.1 reshape_squeeze.6
  3.7 0.8 copy-done.1
  4.5 0.1 copy.11
  4.6 0.1 reshape_squeeze.7
  4.7 0.8 copy_bitcast_fusion
  5.6 138.7 %shard_map.76 = (f32[2,64,640]{2,1,0:T(8,128)}, f32[9,40,128]{2,1,0:T(8,128)}, f32[9,40,128]{2,1,0:T(8,128)}) custom-call(f32[3,2,64,640]{3,2,1,0:T(8,128)} %qkv.1, f32[64,1]{1,0:T(8,128)} %copy.13.eta, f32[9,40,128]{2,1,0:T(8,128)} %get-tuple-element.13.own_w, f32[9,40,128]{2,1,0:T(8,128)} %get-tuple-element.12.own_m, f32[1,640]{1,0:T(1,128)} %reshape.19.gain), custom_call_target="tpu_custom_call" | custom-call | tf_op jit(solution)/shard_map/pallas_call | solution.py:307
  144.3 1.0 copy.14
  145.3 0.1 reshape.20
  145.4 0.0 copy-start.2
  145.4 0.7 copy.16
  146.1 0.3 copy-done.2
  146.4 0.1 copy.15
  146.4 0.1 reshape.21
  146.5 0.0 copy-start
  146.5 0.7 copy.17
  147.2 0.3 copy-done
  147.6 0.7 copy.21
Async XLA Ops:
  0.6 1.3 copy-start.3
  3.6 0.9 copy-start.1
  145.4 1.0 copy-start.2
  146.5 1.0 copy-start
